TPU v7x, 128 devices: a whole 4x4x4 slice. The times are simulated.
128 devices in a mesh: dp: 8 (over z, core), tp: 16 (over y, x).
Axes of the slice: x: 4, y: 4, z: 4, core: 2. Of those that a mesh axis runs over, the one named last changes fastest.
Arguments:
- head_fsdp: bfloat16 [4096, 128256], P(('dp', 'tp')), may hold values from -0.5 to 0.5
- hidden: bfloat16 [2048, 4096], P(('dp', 'tp')), may hold values from -48 to 48
- targets: int32 [2048], P(('dp', 'tp')), may hold values from 0 to 128255
Outputs:
- head_tp: bfloat16 [4096, 128256], P('dp', 'tp')
- log_norm: float32 [2048], P(('dp', 'tp'))
- target_logprob: float32 [2048], P(('dp', 'tp'))
All inputs are finite; a program needn't handle non-finite values.
Results may differ from a plain program's by a relative error of at most 0.0004.
Values may be sent and summed in bfloat16 or wider, within the bound.
No kernel may reach another device: no remote copies, remote signals or barrier semaphores. Data moves between devices by JAX's collectives and lax.ppermute only.
A program may use at most 192 MiB of HBM per device.

v0:
```python
import jax
import jax.numpy as jnp
from jax import lax
from jax.sharding import Mesh
from jax.sharding import PartitionSpec as P

TP = ("tp_0", "tp_1")
DP = ("dp_0", "dp_1")
DP_TP = ("dp_0", "dp_1", "tp_0", "tp_1")


def all_in_one(shard, axis):
    leaves = jax.tree.leaves(shard)
    order = sorted(range(len(leaves)), key=lambda k: -leaves[k].size)
    width = (1, *leaves[order[0]].shape)[-1]
    lines = [
        jnp.pad(leaves[k].reshape(-1), (0, -leaves[k].size % width)).reshape(-1, width)
        for k in order
    ]
    both, at, found = (lax.all_gather(jnp.concatenate(lines), axis), 0, {})
    for k, line in zip(order, lines):
        piece = both[:, at : at + len(line)].reshape(len(both), -1)
        found[k] = piece[:, : leaves[k].size].reshape(-1, *leaves[k].shape)
        at += len(line)
    numbers = iter(range(len(leaves)))
    return jax.tree.map(lambda _: found[next(numbers)], shard)


def joined_all(shard, axes, combine):
    for axis in axes:
        pieces = all_in_one(shard, axis)
        shard = jax.tree.map(lambda part: part[0], pieces)
        for k in range(1, lax.axis_size(axis)):
            shard = combine(shard, jax.tree.map(lambda part: part[k], pieces))
    return shard


def combine_rows(earlier, later):
    peak_one, mass_one, pick_one = earlier
    peak_two, mass_two, pick_two = later
    highest = jnp.maximum(peak_one, peak_two)
    joined = mass_one * jnp.exp(peak_one - highest) + mass_two * jnp.exp(peak_two - highest)
    return (highest, joined, pick_one + pick_two)


def shards(head_fsdp, hidden, targets):
    head_tp = lax.all_to_all(head_fsdp, TP, split_axis=1, concat_axis=0, tiled=True)
    head_full = lax.all_to_all(head_tp, DP, split_axis=1, concat_axis=0, tiled=True)
    vocab_start = lax.axis_index(TP) * head_tp.shape[1] + lax.axis_index(DP) * head_full.shape[1]
    all_hidden, all_targets = (
        lax.all_gather(hidden, DP_TP, axis=0, tiled=True),
        lax.all_gather(targets, DP_TP, axis=0, tiled=True),
    )
    logits = jnp.dot(all_hidden, head_full, preferred_element_type=jnp.float32)
    local_peak = jnp.max(logits, axis=1)
    offset = all_targets - vocab_start
    columns = lax.broadcasted_iota(jnp.int32, logits.shape, 1)
    picked = jnp.sum(jnp.where(columns == offset[:, None], logits, 0.0), axis=1)
    local_mass = jnp.sum(jnp.exp(logits - local_peak[:, None]), axis=1)
    top_logit, total_mass, target_logit = joined_all(
        (local_peak, local_mass, picked), DP_TP, combine_rows
    )
    log_norm = top_logit + jnp.log(total_mass)
    logprob = target_logit - log_norm
    own_rows = hidden.shape[0]
    row_start = (lax.axis_index(DP) * lax.axis_size(TP) + lax.axis_index(TP)) * own_rows
    own_norm = lax.dynamic_slice_in_dim(log_norm, row_start, own_rows, 0)
    own_logprob = lax.dynamic_slice_in_dim(logprob, row_start, own_rows, 0)
    return (head_tp, own_norm, own_logprob)


def solution(mesh):
    split = Mesh(mesh.devices.reshape(4, 2, 4, 4), ("dp_0", "dp_1", "tp_0", "tp_1"))
    placed = (P(DP_TP, None), P(DP_TP, None), P(DP_TP))
    return jax.shard_map(
        shards,
        mesh=split,
        in_specs=placed,
        out_specs=(P(DP, TP), P(DP_TP), P(DP_TP)),
        check_vma=False,
    )
```

profile of v0, /device:TPU:0, one launch (start us, length us, event | category | flops | bytes accessed | tf_op | source)
XLA Modules:
  0.0 437.6 jit_solution(9103793541087411088)
XLA Ops:
  7.2 0.0 all-gather.10.cloned.1.call-start
  7.2 0.7 all-gather.10.cloned.1.call-update
  7.9 14.4 %all_to_all.28 = bf16[32,16,8016]{2,1,0:T(8,128)(2,1)} reshape(bf16[32,128256]{1,0:T(8,128)(2,1)} %param.3) | data formatting | bytes 16416768 | tf_op jit(solution)/shard_map/all_to_all | solution.py:47
  22.3 8.0 %copy.10 = bf16[32,16,8016]{2,0,1:T(8,128)(2,1)} copy(bf16[32,16,8016]{2,1,0:T(8,128)(2,1)} %all_to_all.28) | data formatting | bytes 16416768 | tf_op jit(solution)/shard_map/all_to_all | solution.py:47
  30.3 129.8 %all_to_all.38 = bf16[32,16,8016]{2,0,1:T(8,128)(2,1)} all-to-all(bf16[32,16,8016]{2,0,1:T(8,128)(2,1)} %copy.10), channel_id=1, replica_groups=mesh['dp_0'=4,'dp_1'=2,'tp_0'=4,'tp_1'=4] {'tp_0','tp_1'}, dimensions={1} | all-to-all | bytes 16416768 | tf_op jit(solution)/shard_map/all_to_all | solution.py:47
  160.1 18.6 %all_to_all.32 = bf16[512,8,1002]{2,1,0:T(8,128)(2,1)} reshape(bf16[16,32,8016]{2,1,0:T(8,128)(2,1)} %bitcast.203) | data formatting | bytes 16416768 | tf_op jit(solution)/shard_map/all_to_all | solution.py:48
  178.7 12.5 %copy.11 = bf16[512,8,1002]{0,2,1:T(8,128)(2,1)} copy(bf16[512,8,1002]{2,1,0:T(8,128)(2,1)} %all_to_all.32) | data formatting | bytes 16416768 | tf_op jit(solution)/shard_map/all_to_all | solution.py:48
  191.2 0.0 copy-start
  191.2 5.4 %all-to-all-start.1 = ((bf16[512,8,1002]{0,2,1:T(8,128)(2,1)}), bf16[512,8,1002]{0,2,1:T(8,128)(2,1)}, u32[]{:S(2)}, u32[]{:S(2)}) async-start(bf16[512,8,1002]{0,2,1:T(8,128)(2,1)} %copy.11), calls=%async_computation.1 | async-start | bytes 16515072 | tf_op jit(solution)/shard_map/all_to_all | solution.py:48
  196.6 0.0 copy-done
  196.6 0.3 dynamic-update-slice
  196.9 146.1 %all-reduce = s32[2048]{0:T(1024)S(1)} all-reduce(s32[2048]{0:T(1024)S(1)} %dynamic-update-slice), channel_id=1, replica_groups=mesh['dp_0'=4,'dp_1'=2,'tp_0'=4,'tp_1'=4] {'dp_0','dp_1','tp_0','tp_1'}, use_global_device_ids=true, to_apply=%add | all-reduce | flops 2048 | bytes 16384
  342.9 11.7 %copy.13 = bf16[512,8016]{0,1:T(8,128)(2,1)} copy(bf16[512,8016]{1,0:T(8,128)(2,1)} %bitcast.204) | data formatting | bytes 16416768
  354.6 0.0 all-to-all-done.1
  354.6 12.1 %copy.12 = bf16[8,512,1002]{2,1,0:T(8,128)(2,1)} copy(bf16[8,512,1002]{1,2,0:T(8,128)(2,1)} %bitcast.2) | data formatting | bytes 16416768 | tf_op jit(solution)/shard_map/all_to_all | solution.py:48
  366.8 0.0 all-gather.10.cloned.1.call-done
  366.8 22.6 %fusion.41 = (f32[2048]{0:T(1024)S(1)}, f32[2048,1002]{0,1:T(8,128)S(1)}) fusion(bf16[2048,4096]{1,0:T(8,128)(2,1)} %all-gather.10.cloned.1.call-done, bf16[4096,1002]{1,0:T(8,128)(2,1)} %bitcast.205), kind=kOutput, calls=%fused_computation.81 | convolution fusion | flops 16812820480 | bytes 33202176 | tf_op jit(solution)/shard_map/dot_general | solution.py:54
  389.4 2.3 exponential_reduce_fusion
  391.7 12.0 %all-gather.4 = f32[4,3,2048]{2,1,0:T(4,128)S(1)} all-gather(f32[1,3,2048]{2,1,0:T(4,128)S(1)} %maximum_bitcast_fusion), channel_id=2, replica_groups=mesh['dp_0'=4,'dp_1'=2,'tp_0'=4,'tp_1'=4] {'dp_0'}, dimensions={0}, use_global_device_ids=true | all-gather | bytes 122880 | tf_op jit(solution)/shard_map/all_gather | solution.py:20
  403.8 0.1 fusion.16
  403.9 1.9 all-gather.5
  405.8 12.0 %all-gather.6 = f32[4,3,2048]{2,1,0:T(4,128)S(1)} all-gather(f32[1,3,2048]{2,1,0:T(4,128)S(1)} %maximum_bitcast_fusion.2), channel_id=4, replica_groups=mesh['dp_0'=4,'dp_1'=2,'tp_0'=4,'tp_1'=4] {'tp_0'}, dimensions={0}, use_global_device_ids=true | all-gather | bytes 122880 | tf_op jit(solution)/shard_map/all_gather | solution.py:20
  417.9 0.1 fusion.2
  418.0 12.0 %all-gather.7 = f32[4,3,2048]{2,1,0:T(4,128)S(1)} all-gather(f32[1,3,2048]{2,1,0:T(4,128)S(1)} %maximum_bitcast_fusion.3), channel_id=5, replica_groups=mesh['dp_0'=4,'dp_1'=2,'tp_0'=4,'tp_1'=4] {'tp_1'}, dimensions={0}, use_global_device_ids=true | all-gather | bytes 122880 | tf_op jit(solution)/shard_map/all_gather | solution.py:20
  430.0 0.1 fusion.40
  430.1 0.6 dynamic-slice_subtract_fusion
  (11 shorter events, 0.3 us)
Async XLA Ops:
  7.2 359.6 %all-gather.10.cloned.1.call-start = ((), (), s32[]{:S(2)}) async-start(), calls=%async_computation.2 | async-start | bytes 16908288 | tf_op jit(solution)/shard_map/all_gather | solution.py:51
  191.2 5.4 %copy-start = (s32[16]{0:T(128)S(1)}, s32[16]{0:T(128)}, u32[]{:S(2)}) copy-start(s32[16]{0:T(128)} %param.5) | copy-start | bytes 196
  191.2 163.5 %all-to-all-start.1 = ((bf16[512,8,1002]{0,2,1:T(8,128)(2,1)}), bf16[512,8,1002]{0,2,1:T(8,128)(2,1)}, u32[]{:S(2)}, u32[]{:S(2)}) async-start(bf16[512,8,1002]{0,2,1:T(8,128)(2,1)} %copy.11), calls=%async_computation.1 | async-start | bytes 16515072 | tf_op jit(solution)/shard_map/all_to_all | solution.py:48
Sparse Core Ops, SparseCore 0:
  11.1 148.0 all-gather.9
where the time goes:
time: 439 us; the launch traced here: 438 us
  blocking collectives  314 us (72%)
  local copies, waits for them, and re-layouts  77.6 us (18%)
  matrix products  22.6 us (5%)
  between operations  14.1 us (3%)
  starting transfers between devices  5.43 us (1%)
    unnamed x1, blocking collectives  146 us
    all_to_all x1, blocking collectives, shards(): lax.all_to_all(head_fsdp, TP, split_axis=1, concat_axis=0, tiled=True)  130 us
    all_to_all x3, local copies, waits for them, and re-layouts, shards(): lax.all_to_all(head_tp, DP, split_axis=1, concat_axis=0, tiled=True)  43.2 us
    all_gather x4, blocking collectives, all_in_one(): both, at, found = (lax.all_gather(jnp.concatenate(lines), axis), 0, {})  37.8 us
    dot_general x1, matrix products, shards(): logits = jnp.dot(all_hidden, head_full, preferred_element_type=jnp.float32)  22.6 us
    all_to_all x2, local copies, waits for them, and re-layouts, shards(): lax.all_to_all(head_fsdp, TP, split_axis=1, concat_axis=0, tiled=True)  22.4 us
    unnamed x5, local copies, waits for them, and re-layouts  12 us
  transfers between devices with their start and end apart: 2, of which 0 were waited for; matrix products, arithmetic and copies ran while one was open for 10% of the time, Pallas kernels for 0%

commit v1 on v0

--- a/solution.py
+++ b/solution.py
@@ -44,7 +44,9 @@
 
 
 def shards(head_fsdp, hidden, targets):
-    head_tp = lax.all_to_all(head_fsdp, TP, split_axis=1, concat_axis=0, tiled=True)
+    parts = jnp.split(head_fsdp, lax.axis_size(TP), axis=1)
+    incoming = lax.all_to_all(jnp.stack(parts), TP, 0, 0)
+    head_tp = jnp.concatenate(incoming, axis=0)
     head_full = lax.all_to_all(head_tp, DP, split_axis=1, concat_axis=0, tiled=True)
     vocab_start = lax.axis_index(TP) * head_tp.shape[1] + lax.axis_index(DP) * head_full.shape[1]
     all_hidden, all_targets = (

time: 439 us -> 413 us (0.941)
  blocking collectives: 314 us -> 296 us
  local copies, waits for them, and re-layouts: 77.6 us -> 67.3 us
    all_to_all x2 -> x0, local copies, waits for them, and re-layouts: 22.4 us -> none  [shards(): lax.all_to_all(head_fsdp, TP, split_axis=1, concat_axis=0, tiled=True)]
    all_to_all x1, blocking collectives: 130 us -> 113 us  [shards(): incoming = lax.all_to_all(jnp.stack(parts), TP, 0, 0)]
    unnamed x5 -> x22, local copies, waits for them, and re-layouts: 12 us -> 23.6 us
  transfers between devices with their start and end apart: 2 -> 2, of which waited for: 0 -> 0; matrix products, arithmetic and copies ran while one was open for 10% -> 12% of each run, Pallas kernels for 0% -> 0%
where the time goes in v1:
time: 413 us; the launch traced here: 411 us
  blocking collectives  296 us (72%)
  local copies, waits for them, and re-layouts  67.3 us (16%)
  matrix products  22.9 us (6%)
  between operations  14.2 us (3%)
  starting transfers between devices  6.02 us (1%)
    unnamed x1, blocking collectives  146 us
    all_to_all x1, blocking collectives, shards(): incoming = lax.all_to_all(jnp.stack(parts), TP, 0, 0)  113 us
    all_to_all x3, local copies, waits for them, and re-layouts, shards(): lax.all_to_all(head_tp, DP, split_axis=1, concat_axis=0, tiled=True)  43.5 us
    all_gather x4, blocking collectives, all_in_one(): both, at, found = (lax.all_gather(jnp.concatenate(lines), axis), 0, {})  37.8 us
    unnamed x22, local copies, waits for them, and re-layouts  23.6 us
    dot_general x1, matrix products, shards(): logits = jnp.dot(all_hidden, head_full, preferred_element_type=jnp.float32)  22.9 us
  transfers between devices with their start and end apart: 2, of which 0 were waited for; matrix products, arithmetic and copies ran while one was open for 12% of the time, Pallas kernels for 0%

profile of v1, /device:TPU:0, one launch (start us, length us, event | category | flops | bytes accessed | tf_op | source)
XLA Modules:
  0.0 410.9 jit_solution(10634856548962990820)
XLA Ops:
  7.2 0.0 all-gather.10.cloned.1.call-start
  7.2 0.7 all-gather.10.cloned.1.call-update
  7.9 0.0 copy-start
  7.9 1.2 bitcast_dynamic-update-slice_fusion.15
  9.1 1.5 bitcast_dynamic-update-slice_fusion.14
  10.6 1.3 bitcast_dynamic-update-slice_fusion.13
  11.9 1.3 bitcast_dynamic-update-slice_fusion.12
  13.1 1.3 bitcast_dynamic-update-slice_fusion.11
  14.4 1.3 bitcast_dynamic-update-slice_fusion.10
  15.6 1.3 bitcast_dynamic-update-slice_fusion.9
  16.9 1.3 bitcast_dynamic-update-slice_fusion.8
  18.1 0.0 copy-done
  18.2 0.2 bitcast_dynamic-update-slice_fusion.6
  18.4 0.2 bitcast_dynamic-update-slice_fusion.5
  18.6 0.2 bitcast_dynamic-update-slice_fusion.4
  18.8 0.2 bitcast_dynamic-update-slice_fusion.3
  19.1 0.2 bitcast_dynamic-update-slice_fusion.2
  19.3 0.2 bitcast_dynamic-update-slice_fusion.1
  19.5 0.2 bitcast_dynamic-update-slice_fusion
  19.7 112.8 %all_to_all.24 = bf16[16,32,8016]{2,1,0:T(8,128)(2,1)} all-to-all(bf16[16,32,8016]{2,1,0:T(8,128)(2,1)S(1)} %bitcast_dynamic-update-slice_fusion), channel_id=1, replica_groups=mesh['dp_0'=4,'dp_1'=2,'tp_0'=4,'tp_1'=4] {'tp_0','tp_1'}, dimensions={0} | all-to-all | bytes 16416768 | tf_op jit(solution)/shard_map/all_to_all | solution.py:48
  132.5 18.9 %all_to_all.18 = bf16[512,8,1002]{2,1,0:T(8,128)(2,1)} reshape(bf16[16,32,8016]{2,1,0:T(8,128)(2,1)} %all_to_all.24) | data formatting | bytes 16416768 | tf_op jit(solution)/shard_map/all_to_all | solution.py:50
  151.4 12.5 %copy.9 = bf16[512,8,1002]{0,2,1:T(8,128)(2,1)} copy(bf16[512,8,1002]{2,1,0:T(8,128)(2,1)} %all_to_all.18) | data formatting | bytes 16416768 | tf_op jit(solution)/shard_map/all_to_all | solution.py:50
  163.9 0.0 copy-start.1
  163.9 6.0 %all-to-all-start.1 = ((bf16[512,8,1002]{0,2,1:T(8,128)(2,1)}), bf16[512,8,1002]{0,2,1:T(8,128)(2,1)}, u32[]{:S(2)}, u32[]{:S(2)}) async-start(bf16[512,8,1002]{0,2,1:T(8,128)(2,1)} %copy.9), calls=%async_computation.1 | async-start | bytes 16515072 | tf_op jit(solution)/shard_map/all_to_all | solution.py:50
  169.9 0.0 copy-done.1
  169.9 0.3 dynamic-update-slice
  170.2 145.8 %all-reduce = s32[2048]{0:T(1024)S(1)} all-reduce(s32[2048]{0:T(1024)S(1)} %dynamic-update-slice), channel_id=1, replica_groups=mesh['dp_0'=4,'dp_1'=2,'tp_0'=4,'tp_1'=4] {'dp_0','dp_1','tp_0','tp_1'}, use_global_device_ids=true, to_apply=%add | all-reduce | flops 2048 | bytes 16384
  316.0 11.7 %copy.11 = bf16[512,8016]{0,1:T(8,128)(2,1)} copy(bf16[512,8016]{1,0:T(8,128)(2,1)} %bitcast.242) | data formatting | bytes 16416768
  327.7 0.0 all-to-all-done.1
  327.7 12.2 %copy.10 = bf16[8,512,1002]{2,1,0:T(8,128)(2,1)} copy(bf16[8,512,1002]{1,2,0:T(8,128)(2,1)} %bitcast.17) | data formatting | bytes 16416768 | tf_op jit(solution)/shard_map/all_to_all | solution.py:50
  339.9 0.0 all-gather.10.cloned.1.call-done
  339.9 22.9 %fusion.44 = (f32[2048]{0:T(1024)S(1)}, f32[1002,2048]{1,0:T(8,128)S(1)}) fusion(bf16[4096,1002]{1,0:T(8,128)(2,1)} %bitcast.243, bf16[2048,4096]{1,0:T(8,128)(2,1)} %all-gather.10.cloned.1.call-done), kind=kOutput, calls=%fused_computation.100 | convolution fusion | flops 16812820480 | bytes 33202176 | tf_op jit(solution)/shard_map/dot_general | solution.py:56
  362.8 2.3 fusion.1
  365.1 12.0 %all-gather.4 = f32[4,3,2048]{2,1,0:T(4,128)S(1)} all-gather(f32[1,3,2048]{2,1,0:T(4,128)S(1)} %maximum_bitcast_fusion), channel_id=2, replica_groups=mesh['dp_0'=4,'dp_1'=2,'tp_0'=4,'tp_1'=4] {'dp_0'}, dimensions={0}, use_global_device_ids=true | all-gather | bytes 122880 | tf_op jit(solution)/shard_map/all_gather | solution.py:20
  377.1 0.1 fusion.19
  377.3 1.9 all-gather.5
  379.2 12.0 %all-gather.6 = f32[4,3,2048]{2,1,0:T(4,128)S(1)} all-gather(f32[1,3,2048]{2,1,0:T(4,128)S(1)} %maximum_bitcast_fusion.2), channel_id=4, replica_groups=mesh['dp_0'=4,'dp_1'=2,'tp_0'=4,'tp_1'=4] {'tp_0'}, dimensions={0}, use_global_device_ids=true | all-gather | bytes 122880 | tf_op jit(solution)/shard_map/all_gather | solution.py:20
  391.3 0.1 fusion.5
  391.4 12.0 %all-gather.7 = f32[4,3,2048]{2,1,0:T(4,128)S(1)} all-gather(f32[1,3,2048]{2,1,0:T(4,128)S(1)} %maximum_bitcast_fusion.3), channel_id=5, replica_groups=mesh['dp_0'=4,'dp_1'=2,'tp_0'=4,'tp_1'=4] {'tp_1'}, dimensions={0}, use_global_device_ids=true | all-gather | bytes 122880 | tf_op jit(solution)/shard_map/all_gather | solution.py:20
  403.4 0.1 fusion.43
  403.5 0.6 dynamic-slice_subtract_fusion
  (12 shorter events, 0.3 us)
Async XLA Ops:
  7.2 332.7 %all-gather.10.cloned.1.call-start = ((), (), s32[]{:S(2)}) async-start(), calls=%async_computation.2 | async-start | bytes 16908288 | tf_op jit(solution)/shard_map/all_gather | solution.py:53
  7.9 10.3 %copy-start = (bf16[32,128256]{1,0:T(8,128)(2,1)S(1)}, bf16[32,128256]{1,0:T(8,128)(2,1)}, u32[]{:S(2)}) copy-start(bf16[32,128256]{1,0:T(8,128)(2,1)} %param.3) | copy-start | bytes 24625156
  163.9 6.0 %copy-start.1 = (s32[16]{0:T(128)S(1)}, s32[16]{0:T(128)}, u32[]{:S(2)}) copy-start(s32[16]{0:T(128)} %param.5) | copy-start | bytes 196
  163.9 163.8 %all-to-all-start.1 = ((bf16[512,8,1002]{0,2,1:T(8,128)(2,1)}), bf16[512,8,1002]{0,2,1:T(8,128)(2,1)}, u32[]{:S(2)}, u32[]{:S(2)}) async-start(bf16[512,8,1002]{0,2,1:T(8,128)(2,1)} %copy.9), calls=%async_computation.1 | async-start | bytes 16515072 | tf_op jit(solution)/shard_map/all_to_all | solution.py:50
Sparse Core Ops, SparseCore 0:
  11.1 138.4 all-gather.9
